TPU v7x, 32 devices: a whole 2x2x4 slice. The times are simulated.
32 devices in a mesh: row: 8 (over y, x, core), col: 4 (over z).
Axes of the slice: x: 2, y: 2, z: 4, core: 2. Of those that a mesh axis runs over, the one named last changes fastest.
Arguments:
- temps: bfloat16 [12, 64, 16384], P(None, None, ('row', 'col')), may hold values from -6 to 6
- sensors: int32 [12, 512], replicated, may hold values from 0 to 16383
Outputs:
- corr: bfloat16 [512, 16384], P('col', 'row')
Inputs may be any that keep to these rules, and one draw needn't show every extreme that they name: `sensors`: each entry is a pixel index of its tier; candidates may repeat.
All inputs are finite; a program needn't handle non-finite values.
Results may differ from a plain program's by a relative error of at most 0.001.
Values may be sent and summed in bfloat16 or wider, within the bound.
A program may use at most 64 MiB of HBM per device.

v0:
```python
import jax
import jax.numpy as jnp
from jax import lax
from jax.sharding import PartitionSpec as P


def select_columns(fields, sensor_rows, first_pixel):
    width = fields.shape[2]
    offsets = sensor_rows - first_pixel
    pixel_ids = lax.broadcasted_iota(jnp.int32, (width, sensor_rows.shape[1]), 0)

    def one_tier(pair):
        tier_fields, tier_offsets = pair
        selector = (pixel_ids == tier_offsets[None, :]).astype(jnp.bfloat16)
        return jnp.dot(tier_fields, selector, preferred_element_type=jnp.float32)

    return lax.map(one_tier, (fields, offsets))


def body(temps, sensors):
    col_count = lax.axis_size("col")
    first_pixel = (lax.axis_index("row") * col_count + lax.axis_index("col")) * temps.shape[2]
    local_values = select_columns(temps, sensors, first_pixel)
    owned = lax.psum_scatter(
        local_values.astype(jnp.bfloat16), "col", scatter_dimension=2, tiled=True
    )
    readings = lax.psum(owned, "row").astype(jnp.float32).astype(jnp.bfloat16)
    scale_factor = 1.0 / jnp.sqrt(jnp.float32(temps.shape[0] * temps.shape[1]))
    summed = jnp.einsum(
        "tsc,tsp->cp",
        lax.all_gather(readings, "col", axis=2, tiled=True),
        temps,
        preferred_element_type=jnp.float32,
    )
    rounded = (summed * scale_factor).astype(jnp.bfloat16)
    return lax.all_to_all(rounded, "col", split_axis=0, concat_axis=1, tiled=True)


def solution(mesh):
    placed = (P(None, None, ("row", "col")), P())
    return jax.shard_map(
        body, mesh=mesh, in_specs=placed, out_specs=P("col", "row"), check_vma=False
    )
```

profile of v0, /device:TPU:0, one launch (start us, length us, event | category | flops | bytes accessed | tf_op | source)
XLA Modules:
  0.0 149.4 jit_solution(5405462871860880620)
XLA Ops:
  6.5 0.0 reduce-scatter.4.cloned.1.call-start
  6.5 0.8 broadcast_subtract_fusion
  7.3 14.2 %while.11 = (s32[]{:T(128)}, bf16[12,64,512]{2,1,0:T(8,128)(2,1)S(1)}, bf16[12,64,512]{2,1,0:T(8,128)(2,1)}, s32[12,512]{1,0:T(8,128)S(1)}, s32[]{:T(128)}) while((s32[]{:T(128)}, bf16[12,64,512]{2,1,0:T(8,128)(2,1)S(1)}, bf16[12,64,512]{2,1,0:T(8,128)(2,1)}, s32[12,512]{1,0:T(8,128)S(1)}, s32[]{:T(128)}) %tuple.21), condition=%wide.region_1.2_spmd.clone, body=%wide.region_0.1_spmd.clone.sunk | while | flops 33816576 | bytes 203849 | solution.py:17
  7.3 1.2 fusion.14
  8.5 1.2 fusion.14
  9.7 1.2 fusion.14
  10.9 1.2 fusion.14
  12.1 1.2 fusion.14
  13.2 1.2 fusion.14
  14.4 1.2 fusion.14
  15.6 1.2 fusion.14
  16.8 1.2 fusion.14
  18.0 1.2 fusion.14
  19.2 1.2 fusion.14
  20.4 1.2 fusion.14
  21.5 2.0 %copy.5 = bf16[12,64,512]{1,0,2:T(8,128)(2,1)S(1)} copy(bf16[12,64,512]{2,1,0:T(8,128)(2,1)S(1)} %get-tuple-element.32) | data formatting | bytes 1572864
  23.5 2.0 %reshape.4 = bf16[512,768]{1,0:T(8,128)(2,1)} reshape(bf16[512,12,64]{2,1,0:T(8,128)(2,1)S(1)} %bitcast.28) | data formatting | bytes 1572864
  25.6 0.0 copy-start
  25.6 0.0 reduce-scatter.4.cloned.1.call-update
  25.6 0.0 all-reduce.2.cloned.1.call-start
  25.7 26.0 %reduce-scatter.4.cloned.1.call-done = bf16[128,768]{1,0:T(8,128)(2,1)} async-done(((bf16[512,768]{1,0:T(8,128)(2,1)}), bf16[128,768]{1,0:T(8,128)(2,1)}) %reduce-scatter.4.cloned.1.call-update) | async-done | bytes 196624
  51.7 1.3 reshape.5
  52.9 1.0 copy.6
  54.0 0.0 all-reduce.2.cloned.1.call-update
  54.0 53.9 %all-reduce.2.cloned.1.call-done = bf16[12,64,128]{2,1,0:T(8,128)(2,1)} async-done(((bf16[12,64,128]{2,1,0:T(8,128)(2,1)}), bf16[12,64,128]{2,1,0:T(8,128)(2,1)}) %all-reduce.2.cloned.1.call-update) | async-done | bytes 196624 | tf_op jit(solution)/shard_map/psum | solution.py:27
  107.9 18.8 %all_gather.3 = bf16[12,64,512]{2,1,0:T(8,128)(2,1)S(1)} all-gather(bf16[12,64,128]{2,1,0:T(8,128)(2,1)} %all-reduce.2.cloned.1.call-done), channel_id=1, replica_groups=mesh['row'=8,'col'=4] {'col'}, dimensions={2}, use_global_device_ids=true | all-gather | bytes 983040 | tf_op jit(solution)/shard_map/all_gather | solution.py:31
  126.7 0.0 copy-done
  126.7 0.6 fusion.8
  127.3 14.4 %all_to_all.19 = bf16[4,128,512]{2,1,0:T(8,128)(2,1)S(1)} all-to-all(bf16[4,128,512]{2,1,0:T(8,128)(2,1)S(1)} %bitcast.31), channel_id=1, replica_groups=mesh['row'=8,'col'=4] {'col'}, dimensions={0} | all-to-all | bytes 1048576 | tf_op jit(solution)/shard_map/all_to_all | solution.py:36
  141.8 0.8 copy.7
  (13 shorter events, 0.1 us)
Async XLA Ops:
  6.5 45.1 %reduce-scatter.4.cloned.1.call-start = ((), (), s32[]{:S(2)}) async-start(), calls=%async_computation.3 | async-start | bytes 983040
  25.6 101.2 %copy-start = (bf16[12,64,512]{2,1,0:T(8,128)(2,1)S(1)}, bf16[12,64,512]{2,1,0:T(8,128)(2,1)}, u32[]{:S(2)}) copy-start(bf16[12,64,512]{2,1,0:T(8,128)(2,1)} %get-tuple-element.99) | copy-start | bytes 2359300
  25.6 82.3 %all-reduce.2.cloned.1.call-start = ((), (), s32[]{:S(2)}) async-start(), calls=%async_computation.2 | async-start | bytes 393216 | tf_op jit(solution)/shard_map/psum | solution.py:27
Sparse Core Ops, SparseCore 0:
  25.7 25.8 reduce-scatter.3
  54.7 53.1 all-reduce.1
where the time goes:
time: 150 us; the launch traced here: 149 us
  waiting for transfers between devices  80 us (53%)
  blocking collectives  33.2 us (22%)
  matrix products  14.5 us (10%)
  between operations  13.4 us (9%)
  local copies, waits for them, and re-layouts  7.3 us (5%)
    psum x1, waiting for transfers between devices, body(): readings = lax.psum(owned, 'row').astype(jnp.float32).astype(jnp.bfloat16)  53.9 us
    unnamed x3, waiting for transfers between devices  26 us
    all_gather x1, blocking collectives, body(): lax.all_gather(readings, 'col', axis=2, tiled=True)  18.8 us
    all_to_all x1, blocking collectives, body(): lax.all_to_all(rounded, 'col', split_axis=0, concat_axis=1, tiled=True)  14.4 us
    dot_general x12, matrix products, one_tier(): return jnp.dot(tier_fields, selector, preferred_element_type=jnp.float32)  13.9 us
    unnamed x6, local copies, waits for them, and re-layouts  6.33 us
  transfers between devices with their start and end apart: 2, of which 2 were waited for; matrix products, arithmetic and copies ran while one was open for 0% of the time, Pallas kernels for 0%

commit v1 on v0

--- a/solution.py
+++ b/solution.py
@@ -28,7 +28,9 @@
     scale_factor = 1.0 / jnp.sqrt(jnp.float32(temps.shape[0] * temps.shape[1]))
     summed = jnp.einsum(
         "tsc,tsp->cp",
-        lax.all_gather(readings, "col", axis=2, tiled=True),
+        jnp.concatenate(
+            lax.all_to_all(jnp.stack([readings] * lax.axis_size("col")), "col", 0, 0), axis=2
+        ),
         temps,
         preferred_element_type=jnp.float32,
     )

time: 150 us -> 158 us (1.053)
  blocking collectives: 33.2 us -> 40.2 us
    all_to_all x0 -> x1, blocking collectives: none -> 23.7 us  [body(): lax.all_to_all(jnp.stack([readings] * lax.axis_size('col')), 'col', 0, 0)]
    all_gather x1 -> x0, blocking collectives: 18.8 us -> none  [body(): lax.all_gather(readings, 'col', axis=2, tiled=True)]
    all_to_all x1, blocking collectives: 14.4 us -> 16.5 us  [body(): lax.all_to_all(rounded, 'col', split_axis=0, concat_axis=1, tiled=True)]
where the time goes in v1:
time: 158 us
  waiting for transfers between devices  80 us (51%)
  blocking collectives  40.2 us (25%)
  matrix products  14.5 us (9%)
  between operations  13.4 us (8%)
  local copies, waits for them, and re-layouts  8.4 us (5%)
    psum x1, waiting for transfers between devices, body(): readings = lax.psum(owned, 'row').astype(jnp.float32).astype(jnp.bfloat16)  53.9 us
    unnamed x3, waiting for transfers between devices  26 us
    all_to_all x1, blocking collectives, body(): lax.all_to_all(jnp.stack([readings] * lax.axis_size('col')), 'col', 0, 0)  23.7 us
    all_to_all x1, blocking collectives, body(): lax.all_to_all(rounded, 'col', split_axis=0, concat_axis=1, tiled=True)  16.5 us
    dot_general x12, matrix products, one_tier(): return jnp.dot(tier_fields, selector, preferred_element_type=jnp.float32)  13.9 us
    unnamed x6, local copies, waits for them, and re-layouts  6.34 us
  transfers between devices with their start and end apart: 2, of which 2 were waited for; matrix products, arithmetic and copies ran while one was open for 0% of the time, Pallas kernels for 0%

profile of v1, /device:TPU:0, one launch (start us, length us, event | category | flops | bytes accessed | tf_op | source)
XLA Modules:
  0.0 157.5 jit_solution(1605733432581588166)
XLA Ops:
  6.5 0.0 reduce-scatter.4.cloned.1.call-start
  6.5 0.8 broadcast_subtract_fusion
  7.3 14.2 %while.11 = (s32[]{:T(128)}, bf16[12,64,512]{2,1,0:T(8,128)(2,1)S(1)}, bf16[12,64,512]{2,1,0:T(8,128)(2,1)}, s32[12,512]{1,0:T(8,128)S(1)}, s32[]{:T(128)}) while((s32[]{:T(128)}, bf16[12,64,512]{2,1,0:T(8,128)(2,1)S(1)}, bf16[12,64,512]{2,1,0:T(8,128)(2,1)}, s32[12,512]{1,0:T(8,128)S(1)}, s32[]{:T(128)}) %tuple.21), condition=%wide.region_1.2_spmd.clone, body=%wide.region_0.1_spmd.clone.sunk | while | flops 33816576 | bytes 203849 | solution.py:17
  7.3 1.2 fusion.16
  8.5 1.2 fusion.16
  9.7 1.2 fusion.16
  10.9 1.2 fusion.16
  12.1 1.2 fusion.16
  13.2 1.2 fusion.16
  14.4 1.2 fusion.16
  15.6 1.2 fusion.16
  16.8 1.2 fusion.16
  18.0 1.2 fusion.16
  19.2 1.2 fusion.16
  20.4 1.2 fusion.16
  21.5 2.0 %copy.6 = bf16[12,64,512]{1,0,2:T(8,128)(2,1)S(1)} copy(bf16[12,64,512]{2,1,0:T(8,128)(2,1)S(1)} %get-tuple-element.32) | data formatting | bytes 1572864
  23.5 2.0 %reshape.14 = bf16[512,768]{1,0:T(8,128)(2,1)} reshape(bf16[512,12,64]{2,1,0:T(8,128)(2,1)S(1)} %bitcast.35) | data formatting | bytes 1572864
  25.6 0.0 reduce-scatter.4.cloned.1.call-update
  25.6 0.0 copy-start
  25.6 0.0 all-reduce.2.cloned.1.call-start
  25.7 26.0 %reduce-scatter.4.cloned.1.call-done = bf16[128,768]{1,0:T(8,128)(2,1)} async-done(((bf16[512,768]{1,0:T(8,128)(2,1)}), bf16[128,768]{1,0:T(8,128)(2,1)}) %reduce-scatter.4.cloned.1.call-update) | async-done | bytes 196624
  51.7 1.3 reshape.15
  52.9 1.0 copy.7
  54.0 0.0 all-reduce.2.cloned.1.call-update
  54.0 53.9 %all-reduce.2.cloned.1.call-done = bf16[12,64,128]{2,1,0:T(8,128)(2,1)} async-done(((bf16[12,64,128]{2,1,0:T(8,128)(2,1)}), bf16[12,64,128]{2,1,0:T(8,128)(2,1)}) %all-reduce.2.cloned.1.call-update) | async-done | bytes 196624 | tf_op jit(solution)/shard_map/psum | solution.py:27
  107.9 1.1 stack.2
  109.0 23.7 %all_to_all.24 = bf16[4,12,64,128]{3,2,1,0:T(8,128)(2,1)S(1)} all-to-all(bf16[4,12,64,128]{3,2,1,0:T(8,128)(2,1)S(1)} %stack.2), channel_id=1, replica_groups=mesh['row'=8,'col'=4] {'col'}, dimensions={0} | all-to-all | bytes 1572864 | tf_op jit(solution)/shard_map/all_to_all | solution.py:32
  132.7 0.0 copy-done
  132.7 0.6 fusion.8
  133.3 16.5 %all_to_all.25 = bf16[4,128,512]{2,1,0:T(8,128)(2,1)S(1)} all-to-all(bf16[4,128,512]{2,1,0:T(8,128)(2,1)S(1)} %bitcast.38), channel_id=1, replica_groups=mesh['row'=8,'col'=4] {'col'}, dimensions={0} | all-to-all | bytes 1048576 | tf_op jit(solution)/shard_map/all_to_all | solution.py:38
  149.8 0.8 copy.9
  (13 shorter events, 0.1 us)
Async XLA Ops:
  6.5 45.1 %reduce-scatter.4.cloned.1.call-start = ((), (), s32[]{:S(2)}) async-start(), calls=%async_computation.4 | async-start | bytes 983040
  25.6 107.1 %copy-start = (bf16[12,64,512]{2,1,0:T(8,128)(2,1)S(1)}, bf16[12,64,512]{2,1,0:T(8,128)(2,1)}, u32[]{:S(2)}) copy-start(bf16[12,64,512]{2,1,0:T(8,128)(2,1)} %get-tuple-element.99) | copy-start | bytes 2359300
  25.6 82.3 %all-reduce.2.cloned.1.call-start = ((), (), s32[]{:S(2)}) async-start(), calls=%async_computation.3 | async-start | bytes 393216 | tf_op jit(solution)/shard_map/psum | solution.py:27
Sparse Core Ops, SparseCore 0:
  25.7 25.8 reduce-scatter.3
  54.7 53.1 all-reduce.1
